TPU v7x, 32 devices: a whole 2x2x4 slice. The times are simulated.
32 devices in a mesh: gx: 4 (over z), gy: 4 (over x, core), gz: 2 (over y).
Axes of the slice: x: 2, y: 2, z: 4, core: 2. Of those that a mesh axis runs over, the one named last changes fastest.
Arguments:
- residual: float32 [32, 32, 256], P('gx', 'gy', 'gz'), may hold values from -18 to 18
- direction: float32 [32, 32, 256], P('gx', 'gy', 'gz'), may hold values from -18 to 18
Outputs:
- powers: float32 [2, 4, 32, 32, 256], P(None, None, 'gx', 'gy', 'gz')
- gram_matrix: float32 [9, 9], replicated
- projections: float32 [9], replicated
All inputs are finite; a program needn't handle non-finite values.
Results may differ from a plain program's by a relative error of at most 0.00029.
Values sent between devices are 32-bit elements; how exact they have to be, the bound alone decides.
A program may use at most 64 MiB of HBM per device.

v0:
```python
import jax
import jax.numpy as jnp
from jax import lax
from jax.sharding import PartitionSpec as P

STEPS = 4
MARGIN = 1
SWEEPS = 3
SWEEP_SCALE = 1.0 / 9.0


def extended(cells, sides, width):
    for axis, dim in sides:
        count = lax.axis_size(axis)
        ends = count - 1
        head = lax.slice_in_dim(cells, 0, width, axis=dim)
        tail = lax.slice_in_dim(cells, cells.shape[dim] - width, cells.shape[dim], axis=dim)
        cells = jnp.concatenate(
            [
                lax.ppermute(tail, axis, [(i, (i + 1) % count) for i in range(ends)]),
                cells,
                lax.ppermute(head, axis, [((i + 1) % count, i) for i in range(ends)]),
            ],
            axis=dim,
        )
    return cells


def stencil_image(padded):
    center = padded[:, 1:-1, 1:-1, 1:-1]
    beside = padded[:, 2:, 1:-1, 1:-1] + padded[:, :-2, 1:-1, 1:-1]
    beside = beside + padded[:, 1:-1, 2:, 1:-1] + padded[:, 1:-1, :-2, 1:-1]
    beside = beside + padded[:, 1:-1, 1:-1, 2:] + padded[:, 1:-1, 1:-1, :-2]
    return 6.0 * center - beside


def pad_along(values, dimension, before, after):
    widths = [(0, 0)] * values.ndim
    widths[dimension] = (before, after)
    return jnp.pad(values, widths)


def assemble(received, reach, growth):
    for dimension in (1, 2, 3):
        length = received.shape[dimension] - 2 * reach
        result_len = length + 2 * growth
        middle = lax.slice_in_dim(received, reach, reach + length, axis=dimension)
        middle = pad_along(middle, dimension, growth, growth)
        below_part = lax.slice_in_dim(received, 0, reach, axis=dimension)
        above_part = lax.slice_in_dim(received, reach + length, 2 * reach + length, axis=dimension)
        received = (
            middle
            + pad_along(below_part, dimension, 0, result_len - reach)
            + pad_along(above_part, dimension, result_len - reach, 0)
        )
    return received


def inside_profile(position, cells, devices, margin):
    global_spots = position * cells - margin + jnp.arange(cells + 2 * margin, dtype=jnp.int32)
    return jnp.logical_and(global_spots >= 0, global_spots < devices * cells).astype(jnp.float32)


def grid_mask(cells_x, cells_y, cells_z, margin):
    along_x = inside_profile(lax.axis_index("gx"), cells_x, lax.axis_size("gx"), margin)
    along_y = inside_profile(lax.axis_index("gy"), cells_y, lax.axis_size("gy"), margin)
    along_z = inside_profile(lax.axis_index("gz"), cells_z, lax.axis_size("gz"), margin)
    return along_x[:, None, None] * along_y[None, :, None] * along_z[None, None, :]


def subdomain_solve(source, mask):
    source = mask * source
    iterate = mask * (SWEEP_SCALE * source)
    for sweep_index in range(SWEEPS - 1):
        padded = jnp.pad(iterate, ((0, 0), (1, 1), (1, 1), (1, 1)))
        iterate = mask * (iterate + SWEEP_SCALE * (source - stencil_image(padded)))
    return iterate


def flatten_rows(fields):
    return jnp.stack([member_field.reshape(-1) for member_field in fields])


def inner_table(left_rows, right_rows):
    return jnp.einsum("ac,bc->ab", left_rows, right_rows, precision=lax.Precision.HIGHEST)


def inner_vector(left_rows, target):
    return jnp.einsum("ac,c->a", left_rows, target, precision=lax.Precision.HIGHEST)


def local(residual, direction):
    margin = MARGIN
    cells_x, cells_y, cells_z = residual.shape
    mask = grid_mask(cells_x, cells_y, cells_z, margin)
    cell_count = float(
        lax.axis_size("gx")
        * cells_x
        * lax.axis_size("gy")
        * cells_y
        * lax.axis_size("gz")
        * cells_z
    )
    target = residual.reshape(-1)
    pieces = jnp.pad(
        jnp.stack([direction, residual]),
        ((0, 0), (margin, margin), (margin, margin), (margin, margin)),
    )
    p_fields, p_images, z_fields, z_images = ([], [], [], [])
    for step_index in range(STEPS + 1):
        final_step = step_index == STEPS
        source = None
        deep_reach = 2 * margin + 1
        received = extended(pieces, (("gx", 1), ("gy", 2), ("gz", 3)), deep_reach)
        region = assemble(received, deep_reach, 1)
        fields = region[
            :,
            margin + 1 : margin + 1 + cells_x,
            margin + 1 : margin + 1 + cells_y,
            margin + 1 : margin + 1 + cells_z,
        ]
        if final_step:
            own_images = stencil_image(
                region[
                    :,
                    margin : margin + cells_x + 2,
                    margin : margin + cells_y + 2,
                    margin : margin + cells_z + 2,
                ]
            )
        else:
            wide_images = stencil_image(region)
            own_images = wide_images[
                :, margin : margin + cells_x, margin : margin + cells_y, margin : margin + cells_z
            ]
            if step_index == 0:
                source = jnp.stack([wide_images[0], region[1, 1:-1, 1:-1, 1:-1]])
            else:
                source = wide_images
        p_fields.append(fields[0])
        p_images.append(own_images[0])
        if step_index > 0:
            z_fields.append(fields[1])
            z_images.append(own_images[1])
        if not final_step:
            pieces = subdomain_solve(source, mask)
    basis_rows = flatten_rows(p_fields + z_fields)
    image_rows = flatten_rows(p_images + z_images)
    gram_sum, projection_sum = lax.psum(
        (inner_table(basis_rows, image_rows), inner_vector(basis_rows, target)), ("gx", "gy", "gz")
    )
    powers = jnp.stack([jnp.stack(p_fields[1:]), jnp.stack(z_fields)])
    return (powers, gram_sum / cell_count, projection_sum / cell_count)


def solution(mesh):
    placed = (P("gx", "gy", "gz"), P("gx", "gy", "gz"))
    return jax.shard_map(
        local,
        mesh=mesh,
        in_specs=placed,
        out_specs=(P(None, None, "gx", "gy", "gz"), P(), P()),
        check_vma=False,
    )
```

profile of v0, /device:TPU:14, one launch (start us, length us, event | category | flops | bytes accessed | tf_op | source)
XLA Modules:
  0.0 197.7 jit_solution(4123972771521606894)
XLA Ops:
  1.6 3.5 %collective-permute-start = (f32[2,3,10,130]{3,2,1,0:T(8,128)S(1)}, f32[2,3,10,130]{3,2,1,0:T(8,128)S(1)}, u32[]{:S(2)}, u32[]{:S(2)}) collective-permute-start(f32[2,3,10,130]{3,2,1,0:T(8,128)S(1)} %get-tuple-element.53), channel_id=1, source_target_pairs={{0,8},{8,16},{16,24},{1,9},{9,17},{17,25},{2,10},{10,18},{18,26},{... | collective-permute-start | bytes 93608 | tf_op jit(solution)/shard_map/ppermute | solution.py:20
  5.1 2.4 %collective-permute-start.1 = (f32[2,3,10,130]{3,2,1,0:T(8,128)S(1)}, f32[2,3,10,130]{3,2,1,0:T(8,128)S(1)}, u32[]{:S(2)}, u32[]{:S(2)}) collective-permute-start(f32[2,3,10,130]{3,2,1,0:T(8,128)S(1)} %get-tuple-element.54), channel_id=1, source_target_pairs={{8,0},{16,8},{24,16},{9,1},{17,9},{25,17},{10,2},{18,10},{26,18},{... | collective-permute-start | bytes 93608 | tf_op jit(solution)/shard_map/ppermute | solution.py:22
  8.1 3.5 %collective-permute-done.1 = f32[2,3,10,130]{3,2,1,0:T(8,128)S(1)} collective-permute-done((f32[2,3,10,130]{3,2,1,0:T(8,128)S(1)}, f32[2,3,10,130]{3,2,1,0:T(8,128)S(1)}, u32[]{:S(2)}, u32[]{:S(2)}) %collective-permute-start.1) | collective-permute-done | bytes 31232 | tf_op jit(solution)/shard_map/ppermute | solution.py:22
  11.6 1.9 collective-permute-start.2
  13.6 3.6 %collective-permute-start.3 = (f32[2,16,3,130]{3,2,1,0:T(4,128)S(1)}, f32[2,16,3,130]{3,2,1,0:T(4,128)S(1)}, u32[]{:S(2)}, u32[]{:S(2)}) collective-permute-start(f32[2,16,3,130]{3,2,1,0:T(4,128)S(1)} %get-tuple-element.30), channel_id=1, source_target_pairs={{2,0},{4,2},{6,4},{3,1},{5,3},{7,5},{10,8},{12,10},{14,12},{11,9},... | collective-permute-start | bytes 149768 | tf_op jit(solution)/shard_map/ppermute | solution.py:22
  21.3 4.6 %collective-permute-start.5 = (f32[2,16,16,3]{3,2,1,0:T(8,128)S(1)}, f32[2,16,16,3]{3,2,1,0:T(8,128)S(1)}, u32[]{:S(2)}, u32[]{:S(2)}) collective-permute-start(f32[2,16,16,3]{3,2,1,0:T(8,128)S(1)} %get-tuple-element.28), channel_id=1, source_target_pairs={{1,0},{3,2},{5,4},{7,6},{9,8},{11,10},{13,12},{15,14},{17,16},{19,... | collective-permute-start | bytes 18440 | tf_op jit(solution)/shard_map/ppermute | solution.py:22
  26.0 2.3 %collective-permute-done.4 = f32[2,16,16,3]{3,2,1,0:T(8,128)S(1)} collective-permute-done((f32[2,16,16,3]{3,2,1,0:T(8,128)S(1)}, f32[2,16,16,3]{3,2,1,0:T(8,128)S(1)}, u32[]{:S(2)}, u32[]{:S(2)}) %collective-permute-start.4) | collective-permute-done | bytes 6176 | tf_op jit(solution)/shard_map/ppermute | solution.py:20
  33.6 3.5 %collective-permute-start.6 = (f32[2,3,10,130]{3,2,1,0:T(8,128)S(1)}, f32[2,3,10,130]{3,2,1,0:T(8,128)S(1)}, u32[]{:S(2)}, u32[]{:S(2)}) collective-permute-start(f32[2,3,10,130]{3,2,1,0:T(8,128)S(1)} %get-tuple-element.51), channel_id=1, source_target_pairs={{0,8},{8,16},{16,24},{1,9},{9,17},{17,25},{2,10},{10,18},{18,26},{... | collective-permute-start | bytes 93608 | tf_op jit(solution)/shard_map/ppermute | solution.py:20
  37.1 2.4 %collective-permute-start.7 = (f32[2,3,10,130]{3,2,1,0:T(8,128)S(1)}, f32[2,3,10,130]{3,2,1,0:T(8,128)S(1)}, u32[]{:S(2)}, u32[]{:S(2)}) collective-permute-start(f32[2,3,10,130]{3,2,1,0:T(8,128)S(1)} %get-tuple-element.52), channel_id=1, source_target_pairs={{8,0},{16,8},{24,16},{9,1},{17,9},{25,17},{10,2},{18,10},{26,18},{... | collective-permute-start | bytes 93608 | tf_op jit(solution)/shard_map/ppermute | solution.py:22
  40.1 3.5 %collective-permute-done.7 = f32[2,3,10,130]{3,2,1,0:T(8,128)S(1)} collective-permute-done((f32[2,3,10,130]{3,2,1,0:T(8,128)S(1)}, f32[2,3,10,130]{3,2,1,0:T(8,128)S(1)}, u32[]{:S(2)}, u32[]{:S(2)}) %collective-permute-start.7) | collective-permute-done | bytes 31232 | tf_op jit(solution)/shard_map/ppermute | solution.py:22
  43.7 1.9 collective-permute-start.8
  45.6 3.6 %collective-permute-start.9 = (f32[2,16,3,130]{3,2,1,0:T(4,128)S(1)}, f32[2,16,3,130]{3,2,1,0:T(4,128)S(1)}, u32[]{:S(2)}, u32[]{:S(2)}) collective-permute-start(f32[2,16,3,130]{3,2,1,0:T(4,128)S(1)} %get-tuple-element.26), channel_id=1, source_target_pairs={{2,0},{4,2},{6,4},{3,1},{5,3},{7,5},{10,8},{12,10},{14,12},{11,9},... | collective-permute-start | bytes 149768 | tf_op jit(solution)/shard_map/ppermute | solution.py:22
  53.3 4.6 %collective-permute-start.11 = (f32[2,16,16,3]{3,2,1,0:T(8,128)S(1)}, f32[2,16,16,3]{3,2,1,0:T(8,128)S(1)}, u32[]{:S(2)}, u32[]{:S(2)}) collective-permute-start(f32[2,16,16,3]{3,2,1,0:T(8,128)S(1)} %get-tuple-element.24), channel_id=1, source_target_pairs={{1,0},{3,2},{5,4},{7,6},{9,8},{11,10},{13,12},{15,14},{17,16},{19,... | collective-permute-start | bytes 18440 | tf_op jit(solution)/shard_map/ppermute | solution.py:22
  57.9 2.4 %collective-permute-done.10 = f32[2,16,16,3]{3,2,1,0:T(8,128)S(1)} collective-permute-done((f32[2,16,16,3]{3,2,1,0:T(8,128)S(1)}, f32[2,16,16,3]{3,2,1,0:T(8,128)S(1)}, u32[]{:S(2)}, u32[]{:S(2)}) %collective-permute-start.10) | collective-permute-done | bytes 6176 | tf_op jit(solution)/shard_map/ppermute | solution.py:20
  64.3 1.9 collective-permute-start.12
  66.3 3.9 %collective-permute-start.13 = (f32[2,3,10,130]{3,2,1,0:T(8,128)S(1)}, f32[2,3,10,130]{3,2,1,0:T(8,128)S(1)}, u32[]{:S(2)}, u32[]{:S(2)}) collective-permute-start(f32[2,3,10,130]{3,2,1,0:T(8,128)S(1)} %get-tuple-element.50), channel_id=1, source_target_pairs={{8,0},{16,8},{24,16},{9,1},{17,9},{25,17},{10,2},{18,10},{26,18},{... | collective-permute-start | bytes 93608 | tf_op jit(solution)/shard_map/ppermute | solution.py:22
  70.9 1.9 collective-permute-done.13
  74.8 3.6 %collective-permute-start.15 = (f32[2,16,3,130]{3,2,1,0:T(4,128)S(1)}, f32[2,16,3,130]{3,2,1,0:T(4,128)S(1)}, u32[]{:S(2)}, u32[]{:S(2)}) collective-permute-start(f32[2,16,3,130]{3,2,1,0:T(4,128)S(1)} %get-tuple-element.22), channel_id=1, source_target_pairs={{2,0},{4,2},{6,4},{3,1},{5,3},{7,5},{10,8},{12,10},{14,12},{11,9},... | collective-permute-start | bytes 149768 | tf_op jit(solution)/shard_map/ppermute | solution.py:22
  82.5 4.6 %collective-permute-start.17 = (f32[2,16,16,3]{3,2,1,0:T(8,128)S(1)}, f32[2,16,16,3]{3,2,1,0:T(8,128)S(1)}, u32[]{:S(2)}, u32[]{:S(2)}) collective-permute-start(f32[2,16,16,3]{3,2,1,0:T(8,128)S(1)} %get-tuple-element.20), channel_id=1, source_target_pairs={{1,0},{3,2},{5,4},{7,6},{9,8},{11,10},{13,12},{15,14},{17,16},{19,... | collective-permute-start | bytes 18440 | tf_op jit(solution)/shard_map/ppermute | solution.py:22
  87.2 2.2 %collective-permute-done.16 = f32[2,16,16,3]{3,2,1,0:T(8,128)S(1)} collective-permute-done((f32[2,16,16,3]{3,2,1,0:T(8,128)S(1)}, f32[2,16,16,3]{3,2,1,0:T(8,128)S(1)}, u32[]{:S(2)}, u32[]{:S(2)}) %collective-permute-start.16) | collective-permute-done | bytes 6176 | tf_op jit(solution)/shard_map/ppermute | solution.py:20
  95.4 3.9 %collective-permute-start.19 = (f32[2,3,10,130]{3,2,1,0:T(8,128)S(1)}, f32[2,3,10,130]{3,2,1,0:T(8,128)S(1)}, u32[]{:S(2)}, u32[]{:S(2)}) collective-permute-start(f32[2,3,10,130]{3,2,1,0:T(8,128)S(1)} %get-tuple-element.48), channel_id=1, source_target_pairs={{8,0},{16,8},{24,16},{9,1},{17,9},{25,17},{10,2},{18,10},{26,18},{... | collective-permute-start | bytes 93608 | tf_op jit(solution)/shard_map/ppermute | solution.py:22
  100.0 1.9 collective-permute-done.19
  102.0 1.9 collective-permute-start.20
  103.9 3.6 %collective-permute-start.21 = (f32[2,16,3,130]{3,2,1,0:T(4,128)S(1)}, f32[2,16,3,130]{3,2,1,0:T(4,128)S(1)}, u32[]{:S(2)}, u32[]{:S(2)}) collective-permute-start(f32[2,16,3,130]{3,2,1,0:T(4,128)S(1)} %get-tuple-element.18), channel_id=1, source_target_pairs={{2,0},{4,2},{6,4},{3,1},{5,3},{7,5},{10,8},{12,10},{14,12},{11,9},... | collective-permute-start | bytes 149768 | tf_op jit(solution)/shard_map/ppermute | solution.py:22
  111.6 4.8 %collective-permute-start.23 = (f32[2,16,16,3]{3,2,1,0:T(8,128)S(1)}, f32[2,16,16,3]{3,2,1,0:T(8,128)S(1)}, u32[]{:S(2)}, u32[]{:S(2)}) collective-permute-start(f32[2,16,16,3]{3,2,1,0:T(8,128)S(1)} %get-tuple-element.16), channel_id=1, source_target_pairs={{1,0},{3,2},{5,4},{7,6},{9,8},{11,10},{13,12},{15,14},{17,16},{19,... | collective-permute-start | bytes 18440 | tf_op jit(solution)/shard_map/ppermute | solution.py:22
  116.5 2.1 %collective-permute-done.22 = f32[2,16,16,3]{3,2,1,0:T(8,128)S(1)} collective-permute-done((f32[2,16,16,3]{3,2,1,0:T(8,128)S(1)}, f32[2,16,16,3]{3,2,1,0:T(8,128)S(1)}, u32[]{:S(2)}, u32[]{:S(2)}) %collective-permute-start.22) | collective-permute-done | bytes 6176 | tf_op jit(solution)/shard_map/ppermute | solution.py:20
  124.6 3.9 %collective-permute-start.25 = (f32[2,3,10,130]{3,2,1,0:T(8,128)S(1)}, f32[2,3,10,130]{3,2,1,0:T(8,128)S(1)}, u32[]{:S(2)}, u32[]{:S(2)}) collective-permute-start(f32[2,3,10,130]{3,2,1,0:T(8,128)S(1)} %get-tuple-element.46), channel_id=1, source_target_pairs={{8,0},{16,8},{24,16},{9,1},{17,9},{25,17},{10,2},{18,10},{26,18},{... | collective-permute-start | bytes 93608 | tf_op jit(solution)/shard_map/ppermute | solution.py:22
  129.2 1.9 collective-permute-done.25
  133.1 3.6 %collective-permute-start.27 = (f32[2,16,3,130]{3,2,1,0:T(4,128)S(1)}, f32[2,16,3,130]{3,2,1,0:T(4,128)S(1)}, u32[]{:S(2)}, u32[]{:S(2)}) collective-permute-start(f32[2,16,3,130]{3,2,1,0:T(4,128)S(1)} %get-tuple-element.14), channel_id=1, source_target_pairs={{2,0},{4,2},{6,4},{3,1},{5,3},{7,5},{10,8},{12,10},{14,12},{11,9},... | collective-permute-start | bytes 149768 | tf_op jit(solution)/shard_map/ppermute | solution.py:22
  140.8 4.6 %collective-permute-start.29 = (f32[2,16,16,3]{3,2,1,0:T(8,128)S(1)}, f32[2,16,16,3]{3,2,1,0:T(8,128)S(1)}, u32[]{:S(2)}, u32[]{:S(2)}) collective-permute-start(f32[2,16,16,3]{3,2,1,0:T(8,128)S(1)} %get-tuple-element.12), channel_id=1, source_target_pairs={{1,0},{3,2},{5,4},{7,6},{9,8},{11,10},{13,12},{15,14},{17,16},{19,... | collective-permute-start | bytes 18440 | tf_op jit(solution)/shard_map/ppermute | solution.py:22
  145.5 2.3 %collective-permute-done.28 = f32[2,16,16,3]{3,2,1,0:T(8,128)S(1)} collective-permute-done((f32[2,16,16,3]{3,2,1,0:T(8,128)S(1)}, f32[2,16,16,3]{3,2,1,0:T(8,128)S(1)}, u32[]{:S(2)}, u32[]{:S(2)}) %collective-permute-start.28) | collective-permute-done | bytes 6176 | tf_op jit(solution)/shard_map/ppermute | solution.py:20
  153.3 42.5 %all-reduce.39 = (f32[9,9]{1,0:T(8,128)S(1)}, f32[9]{0:T(128)S(1)}) all-reduce(f32[9,9]{1,0:T(8,128)S(1)} %fusion.151, f32[9]{0:T(128)S(1)} %convolution_bitcast_fusion), channel_id=1, replica_groups=mesh['gx'=4,'gy'=4,'gz'=2] {'gx','gy','gz'}, use_global_device_ids=true, to_apply=%region_0.1 | all-reduce | flops 90 | bytes 720 | tf_op jit(solution)/shard_map/psum | solution.py:149
  (140 shorter events, 57.2 us)
Async XLA Ops:
  1.6 6.5 %collective-permute-start = (f32[2,3,10,130]{3,2,1,0:T(8,128)S(1)}, f32[2,3,10,130]{3,2,1,0:T(8,128)S(1)}, u32[]{:S(2)}, u32[]{:S(2)}) collective-permute-start(f32[2,3,10,130]{3,2,1,0:T(8,128)S(1)} %get-tuple-element.53), channel_id=1, source_target_pairs={{0,8},{8,16},{16,24},{1,9},{9,17},{17,25},{2,10},{10,18},{18,26},{... | collective-permute-start | bytes 93608 | tf_op jit(solution)/shard_map/ppermute | solution.py:20
  5.1 6.5 %collective-permute-start.1 = (f32[2,3,10,130]{3,2,1,0:T(8,128)S(1)}, f32[2,3,10,130]{3,2,1,0:T(8,128)S(1)}, u32[]{:S(2)}, u32[]{:S(2)}) collective-permute-start(f32[2,3,10,130]{3,2,1,0:T(8,128)S(1)} %get-tuple-element.54), channel_id=1, source_target_pairs={{8,0},{16,8},{24,16},{9,1},{17,9},{25,17},{10,2},{18,10},{26,18},{... | collective-permute-start | bytes 93608 | tf_op jit(solution)/shard_map/ppermute | solution.py:22
  11.6 6.3 %collective-permute-start.2 = (f32[2,16,3,130]{3,2,1,0:T(4,128)S(1)}, f32[2,16,3,130]{3,2,1,0:T(4,128)S(1)}, u32[]{:S(2)}, u32[]{:S(2)}) collective-permute-start(f32[2,16,3,130]{3,2,1,0:T(4,128)S(1)} %get-tuple-element.29), channel_id=1, source_target_pairs={{0,2},{2,4},{4,6},{1,3},{3,5},{5,7},{8,10},{10,12},{12,14},{9,11},... | collective-permute-start | bytes 149768 | tf_op jit(solution)/shard_map/ppermute | solution.py:20
  13.6 6.1 %collective-permute-start.3 = (f32[2,16,3,130]{3,2,1,0:T(4,128)S(1)}, f32[2,16,3,130]{3,2,1,0:T(4,128)S(1)}, u32[]{:S(2)}, u32[]{:S(2)}) collective-permute-start(f32[2,16,3,130]{3,2,1,0:T(4,128)S(1)} %get-tuple-element.30), channel_id=1, source_target_pairs={{2,0},{4,2},{6,4},{3,1},{5,3},{7,5},{10,8},{12,10},{14,12},{11,9},... | collective-permute-start | bytes 149768 | tf_op jit(solution)/shard_map/ppermute | solution.py:22
  20.0 8.3 %collective-permute-start.4 = (f32[2,16,16,3]{3,2,1,0:T(8,128)S(1)}, f32[2,16,16,3]{3,2,1,0:T(8,128)S(1)}, u32[]{:S(2)}, u32[]{:S(2)}) collective-permute-start(f32[2,16,16,3]{3,2,1,0:T(8,128)S(1)} %get-tuple-element.27), channel_id=1, source_target_pairs={{0,1},{2,3},{4,5},{6,7},{8,9},{10,11},{12,13},{14,15},{16,17},{18,... | collective-permute-start | bytes 18440 | tf_op jit(solution)/shard_map/ppermute | solution.py:20
  21.3 8.4 %collective-permute-start.5 = (f32[2,16,16,3]{3,2,1,0:T(8,128)S(1)}, f32[2,16,16,3]{3,2,1,0:T(8,128)S(1)}, u32[]{:S(2)}, u32[]{:S(2)}) collective-permute-start(f32[2,16,16,3]{3,2,1,0:T(8,128)S(1)} %get-tuple-element.28), channel_id=1, source_target_pairs={{1,0},{3,2},{5,4},{7,6},{9,8},{11,10},{13,12},{15,14},{17,16},{19,... | collective-permute-start | bytes 18440 | tf_op jit(solution)/shard_map/ppermute | solution.py:22
  31.3 0.7 copy-start.2
  33.6 6.5 %collective-permute-start.6 = (f32[2,3,10,130]{3,2,1,0:T(8,128)S(1)}, f32[2,3,10,130]{3,2,1,0:T(8,128)S(1)}, u32[]{:S(2)}, u32[]{:S(2)}) collective-permute-start(f32[2,3,10,130]{3,2,1,0:T(8,128)S(1)} %get-tuple-element.51), channel_id=1, source_target_pairs={{0,8},{8,16},{16,24},{1,9},{9,17},{17,25},{2,10},{10,18},{18,26},{... | collective-permute-start | bytes 93608 | tf_op jit(solution)/shard_map/ppermute | solution.py:20
  37.1 6.5 %collective-permute-start.7 = (f32[2,3,10,130]{3,2,1,0:T(8,128)S(1)}, f32[2,3,10,130]{3,2,1,0:T(8,128)S(1)}, u32[]{:S(2)}, u32[]{:S(2)}) collective-permute-start(f32[2,3,10,130]{3,2,1,0:T(8,128)S(1)} %get-tuple-element.52), channel_id=1, source_target_pairs={{8,0},{16,8},{24,16},{9,1},{17,9},{25,17},{10,2},{18,10},{26,18},{... | collective-permute-start | bytes 93608 | tf_op jit(solution)/shard_map/ppermute | solution.py:22
  43.7 6.3 %collective-permute-start.8 = (f32[2,16,3,130]{3,2,1,0:T(4,128)S(1)}, f32[2,16,3,130]{3,2,1,0:T(4,128)S(1)}, u32[]{:S(2)}, u32[]{:S(2)}) collective-permute-start(f32[2,16,3,130]{3,2,1,0:T(4,128)S(1)} %get-tuple-element.25), channel_id=1, source_target_pairs={{0,2},{2,4},{4,6},{1,3},{3,5},{5,7},{8,10},{10,12},{12,14},{9,11},... | collective-permute-start | bytes 149768 | tf_op jit(solution)/shard_map/ppermute | solution.py:20
  45.6 6.1 %collective-permute-start.9 = (f32[2,16,3,130]{3,2,1,0:T(4,128)S(1)}, f32[2,16,3,130]{3,2,1,0:T(4,128)S(1)}, u32[]{:S(2)}, u32[]{:S(2)}) collective-permute-start(f32[2,16,3,130]{3,2,1,0:T(4,128)S(1)} %get-tuple-element.26), channel_id=1, source_target_pairs={{2,0},{4,2},{6,4},{3,1},{5,3},{7,5},{10,8},{12,10},{14,12},{11,9},... | collective-permute-start | bytes 149768 | tf_op jit(solution)/shard_map/ppermute | solution.py:22
  52.0 8.3 %collective-permute-start.10 = (f32[2,16,16,3]{3,2,1,0:T(8,128)S(1)}, f32[2,16,16,3]{3,2,1,0:T(8,128)S(1)}, u32[]{:S(2)}, u32[]{:S(2)}) collective-permute-start(f32[2,16,16,3]{3,2,1,0:T(8,128)S(1)} %get-tuple-element.23), channel_id=1, source_target_pairs={{0,1},{2,3},{4,5},{6,7},{8,9},{10,11},{12,13},{14,15},{16,17},{18,... | collective-permute-start | bytes 18440 | tf_op jit(solution)/shard_map/ppermute | solution.py:20
  53.3 8.4 %collective-permute-start.11 = (f32[2,16,16,3]{3,2,1,0:T(8,128)S(1)}, f32[2,16,16,3]{3,2,1,0:T(8,128)S(1)}, u32[]{:S(2)}, u32[]{:S(2)}) collective-permute-start(f32[2,16,16,3]{3,2,1,0:T(8,128)S(1)} %get-tuple-element.24), channel_id=1, source_target_pairs={{1,0},{3,2},{5,4},{7,6},{9,8},{11,10},{13,12},{15,14},{17,16},{19,... | collective-permute-start | bytes 18440 | tf_op jit(solution)/shard_map/ppermute | solution.py:22
  64.3 6.5 %collective-permute-start.12 = (f32[2,3,10,130]{3,2,1,0:T(8,128)S(1)}, f32[2,3,10,130]{3,2,1,0:T(8,128)S(1)}, u32[]{:S(2)}, u32[]{:S(2)}) collective-permute-start(f32[2,3,10,130]{3,2,1,0:T(8,128)S(1)} %get-tuple-element.49), channel_id=1, source_target_pairs={{0,8},{8,16},{16,24},{1,9},{9,17},{17,25},{2,10},{10,18},{18,26},{... | collective-permute-start | bytes 93608 | tf_op jit(solution)/shard_map/ppermute | solution.py:20
  66.3 6.5 %collective-permute-start.13 = (f32[2,3,10,130]{3,2,1,0:T(8,128)S(1)}, f32[2,3,10,130]{3,2,1,0:T(8,128)S(1)}, u32[]{:S(2)}, u32[]{:S(2)}) collective-permute-start(f32[2,3,10,130]{3,2,1,0:T(8,128)S(1)} %get-tuple-element.50), channel_id=1, source_target_pairs={{8,0},{16,8},{24,16},{9,1},{17,9},{25,17},{10,2},{18,10},{26,18},{... | collective-permute-start | bytes 93608 | tf_op jit(solution)/shard_map/ppermute | solution.py:22
  72.8 6.3 %collective-permute-start.14 = (f32[2,16,3,130]{3,2,1,0:T(4,128)S(1)}, f32[2,16,3,130]{3,2,1,0:T(4,128)S(1)}, u32[]{:S(2)}, u32[]{:S(2)}) collective-permute-start(f32[2,16,3,130]{3,2,1,0:T(4,128)S(1)} %get-tuple-element.21), channel_id=1, source_target_pairs={{0,2},{2,4},{4,6},{1,3},{3,5},{5,7},{8,10},{10,12},{12,14},{9,11},... | collective-permute-start | bytes 149768 | tf_op jit(solution)/shard_map/ppermute | solution.py:20
  74.8 6.1 %collective-permute-start.15 = (f32[2,16,3,130]{3,2,1,0:T(4,128)S(1)}, f32[2,16,3,130]{3,2,1,0:T(4,128)S(1)}, u32[]{:S(2)}, u32[]{:S(2)}) collective-permute-start(f32[2,16,3,130]{3,2,1,0:T(4,128)S(1)} %get-tuple-element.22), channel_id=1, source_target_pairs={{2,0},{4,2},{6,4},{3,1},{5,3},{7,5},{10,8},{12,10},{14,12},{11,9},... | collective-permute-start | bytes 149768 | tf_op jit(solution)/shard_map/ppermute | solution.py:22
  81.2 8.3 %collective-permute-start.16 = (f32[2,16,16,3]{3,2,1,0:T(8,128)S(1)}, f32[2,16,16,3]{3,2,1,0:T(8,128)S(1)}, u32[]{:S(2)}, u32[]{:S(2)}) collective-permute-start(f32[2,16,16,3]{3,2,1,0:T(8,128)S(1)} %get-tuple-element.19), channel_id=1, source_target_pairs={{0,1},{2,3},{4,5},{6,7},{8,9},{10,11},{12,13},{14,15},{16,17},{18,... | collective-permute-start | bytes 18440 | tf_op jit(solution)/shard_map/ppermute | solution.py:20
  82.5 8.4 %collective-permute-start.17 = (f32[2,16,16,3]{3,2,1,0:T(8,128)S(1)}, f32[2,16,16,3]{3,2,1,0:T(8,128)S(1)}, u32[]{:S(2)}, u32[]{:S(2)}) collective-permute-start(f32[2,16,16,3]{3,2,1,0:T(8,128)S(1)} %get-tuple-element.20), channel_id=1, source_target_pairs={{1,0},{3,2},{5,4},{7,6},{9,8},{11,10},{13,12},{15,14},{17,16},{19,... | collective-permute-start | bytes 18440 | tf_op jit(solution)/shard_map/ppermute | solution.py:22
  93.5 6.5 %collective-permute-start.18 = (f32[2,3,10,130]{3,2,1,0:T(8,128)S(1)}, f32[2,3,10,130]{3,2,1,0:T(8,128)S(1)}, u32[]{:S(2)}, u32[]{:S(2)}) collective-permute-start(f32[2,3,10,130]{3,2,1,0:T(8,128)S(1)} %get-tuple-element.47), channel_id=1, source_target_pairs={{0,8},{8,16},{16,24},{1,9},{9,17},{17,25},{2,10},{10,18},{18,26},{... | collective-permute-start | bytes 93608 | tf_op jit(solution)/shard_map/ppermute | solution.py:20
  95.4 6.5 %collective-permute-start.19 = (f32[2,3,10,130]{3,2,1,0:T(8,128)S(1)}, f32[2,3,10,130]{3,2,1,0:T(8,128)S(1)}, u32[]{:S(2)}, u32[]{:S(2)}) collective-permute-start(f32[2,3,10,130]{3,2,1,0:T(8,128)S(1)} %get-tuple-element.48), channel_id=1, source_target_pairs={{8,0},{16,8},{24,16},{9,1},{17,9},{25,17},{10,2},{18,10},{26,18},{... | collective-permute-start | bytes 93608 | tf_op jit(solution)/shard_map/ppermute | solution.py:22
  102.0 6.3 %collective-permute-start.20 = (f32[2,16,3,130]{3,2,1,0:T(4,128)S(1)}, f32[2,16,3,130]{3,2,1,0:T(4,128)S(1)}, u32[]{:S(2)}, u32[]{:S(2)}) collective-permute-start(f32[2,16,3,130]{3,2,1,0:T(4,128)S(1)} %get-tuple-element.17), channel_id=1, source_target_pairs={{0,2},{2,4},{4,6},{1,3},{3,5},{5,7},{8,10},{10,12},{12,14},{9,11},... | collective-permute-start | bytes 149768 | tf_op jit(solution)/shard_map/ppermute | solution.py:20
  103.9 6.1 %collective-permute-start.21 = (f32[2,16,3,130]{3,2,1,0:T(4,128)S(1)}, f32[2,16,3,130]{3,2,1,0:T(4,128)S(1)}, u32[]{:S(2)}, u32[]{:S(2)}) collective-permute-start(f32[2,16,3,130]{3,2,1,0:T(4,128)S(1)} %get-tuple-element.18), channel_id=1, source_target_pairs={{2,0},{4,2},{6,4},{3,1},{5,3},{7,5},{10,8},{12,10},{14,12},{11,9},... | collective-permute-start | bytes 149768 | tf_op jit(solution)/shard_map/ppermute | solution.py:22
  110.3 8.3 %collective-permute-start.22 = (f32[2,16,16,3]{3,2,1,0:T(8,128)S(1)}, f32[2,16,16,3]{3,2,1,0:T(8,128)S(1)}, u32[]{:S(2)}, u32[]{:S(2)}) collective-permute-start(f32[2,16,16,3]{3,2,1,0:T(8,128)S(1)} %get-tuple-element.15), channel_id=1, source_target_pairs={{0,1},{2,3},{4,5},{6,7},{8,9},{10,11},{12,13},{14,15},{16,17},{18,... | collective-permute-start | bytes 18440 | tf_op jit(solution)/shard_map/ppermute | solution.py:20
  111.6 8.4 %collective-permute-start.23 = (f32[2,16,16,3]{3,2,1,0:T(8,128)S(1)}, f32[2,16,16,3]{3,2,1,0:T(8,128)S(1)}, u32[]{:S(2)}, u32[]{:S(2)}) collective-permute-start(f32[2,16,16,3]{3,2,1,0:T(8,128)S(1)} %get-tuple-element.16), channel_id=1, source_target_pairs={{1,0},{3,2},{5,4},{7,6},{9,8},{11,10},{13,12},{15,14},{17,16},{19,... | collective-permute-start | bytes 18440 | tf_op jit(solution)/shard_map/ppermute | solution.py:22
  122.7 6.5 %collective-permute-start.24 = (f32[2,3,10,130]{3,2,1,0:T(8,128)S(1)}, f32[2,3,10,130]{3,2,1,0:T(8,128)S(1)}, u32[]{:S(2)}, u32[]{:S(2)}) collective-permute-start(f32[2,3,10,130]{3,2,1,0:T(8,128)S(1)} %get-tuple-element.45), channel_id=1, source_target_pairs={{0,8},{8,16},{16,24},{1,9},{9,17},{17,25},{2,10},{10,18},{18,26},{... | collective-permute-start | bytes 93608 | tf_op jit(solution)/shard_map/ppermute | solution.py:20
  124.6 6.5 %collective-permute-start.25 = (f32[2,3,10,130]{3,2,1,0:T(8,128)S(1)}, f32[2,3,10,130]{3,2,1,0:T(8,128)S(1)}, u32[]{:S(2)}, u32[]{:S(2)}) collective-permute-start(f32[2,3,10,130]{3,2,1,0:T(8,128)S(1)} %get-tuple-element.46), channel_id=1, source_target_pairs={{8,0},{16,8},{24,16},{9,1},{17,9},{25,17},{10,2},{18,10},{26,18},{... | collective-permute-start | bytes 93608 | tf_op jit(solution)/shard_map/ppermute | solution.py:22
  131.2 6.3 %collective-permute-start.26 = (f32[2,16,3,130]{3,2,1,0:T(4,128)S(1)}, f32[2,16,3,130]{3,2,1,0:T(4,128)S(1)}, u32[]{:S(2)}, u32[]{:S(2)}) collective-permute-start(f32[2,16,3,130]{3,2,1,0:T(4,128)S(1)} %get-tuple-element.13), channel_id=1, source_target_pairs={{0,2},{2,4},{4,6},{1,3},{3,5},{5,7},{8,10},{10,12},{12,14},{9,11},... | collective-permute-start | bytes 149768 | tf_op jit(solution)/shard_map/ppermute | solution.py:20
  133.1 6.1 %collective-permute-start.27 = (f32[2,16,3,130]{3,2,1,0:T(4,128)S(1)}, f32[2,16,3,130]{3,2,1,0:T(4,128)S(1)}, u32[]{:S(2)}, u32[]{:S(2)}) collective-permute-start(f32[2,16,3,130]{3,2,1,0:T(4,128)S(1)} %get-tuple-element.14), channel_id=1, source_target_pairs={{2,0},{4,2},{6,4},{3,1},{5,3},{7,5},{10,8},{12,10},{14,12},{11,9},... | collective-permute-start | bytes 149768 | tf_op jit(solution)/shard_map/ppermute | solution.py:22
  139.5 8.3 %collective-permute-start.28 = (f32[2,16,16,3]{3,2,1,0:T(8,128)S(1)}, f32[2,16,16,3]{3,2,1,0:T(8,128)S(1)}, u32[]{:S(2)}, u32[]{:S(2)}) collective-permute-start(f32[2,16,16,3]{3,2,1,0:T(8,128)S(1)} %get-tuple-element.11), channel_id=1, source_target_pairs={{0,1},{2,3},{4,5},{6,7},{8,9},{10,11},{12,13},{14,15},{16,17},{18,... | collective-permute-start | bytes 18440 | tf_op jit(solution)/shard_map/ppermute | solution.py:20
  140.8 8.4 %collective-permute-start.29 = (f32[2,16,16,3]{3,2,1,0:T(8,128)S(1)}, f32[2,16,16,3]{3,2,1,0:T(8,128)S(1)}, u32[]{:S(2)}, u32[]{:S(2)}) collective-permute-start(f32[2,16,16,3]{3,2,1,0:T(8,128)S(1)} %get-tuple-element.12), channel_id=1, source_target_pairs={{1,0},{3,2},{5,4},{7,6},{9,8},{11,10},{13,12},{15,14},{17,16},{19,... | collective-permute-start | bytes 18440 | tf_op jit(solution)/shard_map/ppermute | solution.py:22
  151.8 0.8 copy-start
  (1 other events, 0.7 us)
where the time goes:
time: 199 us; the launch traced here: 198 us
  starting transfers between devices  86.5 us (43%)
  waiting for transfers between devices  46.7 us (23%)
  blocking collectives  42.5 us (21%)
  other arithmetic  13.6 us (7%)
  local copies, waits for them, and re-layouts  5.35 us (3%)
    ppermute x15, starting transfers between devices, extended(): lax.ppermute(head, axis, [((i + 1) % count, i) for i in range(ends)])  57.7 us
    psum x1, blocking collectives, local(): lax.psum((inner_table(basis_rows, image_rows), inner_vector(basis_rows, t...  42.5 us
    ppermute x15, waiting for transfers between devices, extended(): lax.ppermute(head, axis, [((i + 1) % count, i) for i in range(ends)])  29.1 us
    ppermute x15, starting transfers between devices, extended(): lax.ppermute(tail, axis, [(i, (i + 1) % count) for i in range(ends)])  28.8 us
    ppermute x15, waiting for transfers between devices, extended(): lax.ppermute(tail, axis, [(i, (i + 1) % count) for i in range(ends)])  17.6 us
  transfers between devices with their start and end apart: 30, of which 30 were waited for; matrix products, arithmetic and copies ran while one was open for 0% of the time, Pallas kernels for 0%

commit v1 on v0

--- a/solution.py
+++ b/solution.py
@@ -146,8 +146,13 @@
             pieces = subdomain_solve(source, mask)
     basis_rows = flatten_rows(p_fields + z_fields)
     image_rows = flatten_rows(p_images + z_images)
-    gram_sum, projection_sum = lax.psum(
-        (inner_table(basis_rows, image_rows), inner_vector(basis_rows, target)), ("gx", "gy", "gz")
+    things_register = lambda array_in, a_name, ax_name: lax.psum(
+        lax.psum(array_in, a_name), ax_name
+    )
+    gram_sum, projection_sum = things_register(
+        (inner_table(basis_rows, image_rows), inner_vector(basis_rows, target)),
+        a_name=("gy", "gz"),
+        ax_name="gx",
     )
     powers = jnp.stack([jnp.stack(p_fields[1:]), jnp.stack(z_fields)])
     return (powers, gram_sum / cell_count, projection_sum / cell_count)

time: 199 us -> 183 us (0.920)
  blocking collectives: 42.5 us -> 25.9 us
    psum x1 -> x2, blocking collectives: 42.5 us -> 25.9 us  [the longest x1 15.3 us: local(): lax.psum(array_in, a_name)]
where the time goes in v1:
time: 183 us; the launch traced here: 181 us
  starting transfers between devices  86.5 us (47%)
  waiting for transfers between devices  46.7 us (26%)
  blocking collectives  25.9 us (14%)
  other arithmetic  13.6 us (7%)
  local copies, waits for them, and re-layouts  5.35 us (3%)
    ppermute x15, starting transfers between devices, extended(): lax.ppermute(head, axis, [((i + 1) % count, i) for i in range(ends)])  57.7 us
    ppermute x15, waiting for transfers between devices, extended(): lax.ppermute(head, axis, [((i + 1) % count, i) for i in range(ends)])  29.1 us
    ppermute x15, starting transfers between devices, extended(): lax.ppermute(tail, axis, [(i, (i + 1) % count) for i in range(ends)])  28.8 us
    ppermute x15, waiting for transfers between devices, extended(): lax.ppermute(tail, axis, [(i, (i + 1) % count) for i in range(ends)])  17.6 us
    psum x1, blocking collectives, local(): lax.psum(array_in, a_name)  15.3 us
    psum x1, blocking collectives, local(): lax.psum(lax.psum(array_in, a_name), ax_name)  10.6 us
  transfers between devices with their start and end apart: 30, of which 30 were waited for; matrix products, arithmetic and copies ran while one was open for 0% of the time, Pallas kernels for 0%

profile of v1, /device:TPU:14, one launch (start us, length us, event | category | flops | bytes accessed | tf_op | source)
XLA Modules:
  0.0 181.0 jit_solution(13081775663867979381)
XLA Ops:
  1.6 3.5 %collective-permute-start = (f32[2,3,10,130]{3,2,1,0:T(8,128)S(1)}, f32[2,3,10,130]{3,2,1,0:T(8,128)S(1)}, u32[]{:S(2)}, u32[]{:S(2)}) collective-permute-start(f32[2,3,10,130]{3,2,1,0:T(8,128)S(1)} %get-tuple-element.55), channel_id=1, source_target_pairs={{0,8},{8,16},{16,24},{1,9},{9,17},{17,25},{2,10},{10,18},{18,26},{... | collective-permute-start | bytes 93608 | tf_op jit(solution)/shard_map/ppermute | solution.py:20
  5.1 2.4 %collective-permute-start.1 = (f32[2,3,10,130]{3,2,1,0:T(8,128)S(1)}, f32[2,3,10,130]{3,2,1,0:T(8,128)S(1)}, u32[]{:S(2)}, u32[]{:S(2)}) collective-permute-start(f32[2,3,10,130]{3,2,1,0:T(8,128)S(1)} %get-tuple-element.56), channel_id=1, source_target_pairs={{8,0},{16,8},{24,16},{9,1},{17,9},{25,17},{10,2},{18,10},{26,18},{... | collective-permute-start | bytes 93608 | tf_op jit(solution)/shard_map/ppermute | solution.py:22
  8.1 3.5 %collective-permute-done.1 = f32[2,3,10,130]{3,2,1,0:T(8,128)S(1)} collective-permute-done((f32[2,3,10,130]{3,2,1,0:T(8,128)S(1)}, f32[2,3,10,130]{3,2,1,0:T(8,128)S(1)}, u32[]{:S(2)}, u32[]{:S(2)}) %collective-permute-start.1) | collective-permute-done | bytes 31232 | tf_op jit(solution)/shard_map/ppermute | solution.py:22
  11.6 1.9 %collective-permute-start.2 = (f32[2,16,3,130]{3,2,1,0:T(4,128)S(1)}, f32[2,16,3,130]{3,2,1,0:T(4,128)S(1)}, u32[]{:S(2)}, u32[]{:S(2)}) collective-permute-start(f32[2,16,3,130]{3,2,1,0:T(4,128)S(1)} %get-tuple-element.31), channel_id=1, source_target_pairs={{0,2},{2,4},{4,6},{1,3},{3,5},{5,7},{8,10},{10,12},{12,14},{9,11},... | collective-permute-start | bytes 149768 | tf_op jit(solution)/shard_map/ppermute | solution.py:20
  13.6 3.6 %collective-permute-start.3 = (f32[2,16,3,130]{3,2,1,0:T(4,128)S(1)}, f32[2,16,3,130]{3,2,1,0:T(4,128)S(1)}, u32[]{:S(2)}, u32[]{:S(2)}) collective-permute-start(f32[2,16,3,130]{3,2,1,0:T(4,128)S(1)} %get-tuple-element.32), channel_id=1, source_target_pairs={{2,0},{4,2},{6,4},{3,1},{5,3},{7,5},{10,8},{12,10},{14,12},{11,9},... | collective-permute-start | bytes 149768 | tf_op jit(solution)/shard_map/ppermute | solution.py:22
  21.3 4.6 %collective-permute-start.5 = (f32[2,16,16,3]{3,2,1,0:T(8,128)S(1)}, f32[2,16,16,3]{3,2,1,0:T(8,128)S(1)}, u32[]{:S(2)}, u32[]{:S(2)}) collective-permute-start(f32[2,16,16,3]{3,2,1,0:T(8,128)S(1)} %get-tuple-element.30), channel_id=1, source_target_pairs={{1,0},{3,2},{5,4},{7,6},{9,8},{11,10},{13,12},{15,14},{17,16},{19,... | collective-permute-start | bytes 18440 | tf_op jit(solution)/shard_map/ppermute | solution.py:22
  26.0 2.3 %collective-permute-done.4 = f32[2,16,16,3]{3,2,1,0:T(8,128)S(1)} collective-permute-done((f32[2,16,16,3]{3,2,1,0:T(8,128)S(1)}, f32[2,16,16,3]{3,2,1,0:T(8,128)S(1)}, u32[]{:S(2)}, u32[]{:S(2)}) %collective-permute-start.4) | collective-permute-done | bytes 6176 | tf_op jit(solution)/shard_map/ppermute | solution.py:20
  33.6 3.5 %collective-permute-start.6 = (f32[2,3,10,130]{3,2,1,0:T(8,128)S(1)}, f32[2,3,10,130]{3,2,1,0:T(8,128)S(1)}, u32[]{:S(2)}, u32[]{:S(2)}) collective-permute-start(f32[2,3,10,130]{3,2,1,0:T(8,128)S(1)} %get-tuple-element.53), channel_id=1, source_target_pairs={{0,8},{8,16},{16,24},{1,9},{9,17},{17,25},{2,10},{10,18},{18,26},{... | collective-permute-start | bytes 93608 | tf_op jit(solution)/shard_map/ppermute | solution.py:20
  37.1 2.4 %collective-permute-start.7 = (f32[2,3,10,130]{3,2,1,0:T(8,128)S(1)}, f32[2,3,10,130]{3,2,1,0:T(8,128)S(1)}, u32[]{:S(2)}, u32[]{:S(2)}) collective-permute-start(f32[2,3,10,130]{3,2,1,0:T(8,128)S(1)} %get-tuple-element.54), channel_id=1, source_target_pairs={{8,0},{16,8},{24,16},{9,1},{17,9},{25,17},{10,2},{18,10},{26,18},{... | collective-permute-start | bytes 93608 | tf_op jit(solution)/shard_map/ppermute | solution.py:22
  40.1 3.5 %collective-permute-done.7 = f32[2,3,10,130]{3,2,1,0:T(8,128)S(1)} collective-permute-done((f32[2,3,10,130]{3,2,1,0:T(8,128)S(1)}, f32[2,3,10,130]{3,2,1,0:T(8,128)S(1)}, u32[]{:S(2)}, u32[]{:S(2)}) %collective-permute-start.7) | collective-permute-done | bytes 31232 | tf_op jit(solution)/shard_map/ppermute | solution.py:22
  43.7 1.9 %collective-permute-start.8 = (f32[2,16,3,130]{3,2,1,0:T(4,128)S(1)}, f32[2,16,3,130]{3,2,1,0:T(4,128)S(1)}, u32[]{:S(2)}, u32[]{:S(2)}) collective-permute-start(f32[2,16,3,130]{3,2,1,0:T(4,128)S(1)} %get-tuple-element.27), channel_id=1, source_target_pairs={{0,2},{2,4},{4,6},{1,3},{3,5},{5,7},{8,10},{10,12},{12,14},{9,11},... | collective-permute-start | bytes 149768 | tf_op jit(solution)/shard_map/ppermute | solution.py:20
  45.6 3.6 %collective-permute-start.9 = (f32[2,16,3,130]{3,2,1,0:T(4,128)S(1)}, f32[2,16,3,130]{3,2,1,0:T(4,128)S(1)}, u32[]{:S(2)}, u32[]{:S(2)}) collective-permute-start(f32[2,16,3,130]{3,2,1,0:T(4,128)S(1)} %get-tuple-element.28), channel_id=1, source_target_pairs={{2,0},{4,2},{6,4},{3,1},{5,3},{7,5},{10,8},{12,10},{14,12},{11,9},... | collective-permute-start | bytes 149768 | tf_op jit(solution)/shard_map/ppermute | solution.py:22
  53.3 4.6 %collective-permute-start.11 = (f32[2,16,16,3]{3,2,1,0:T(8,128)S(1)}, f32[2,16,16,3]{3,2,1,0:T(8,128)S(1)}, u32[]{:S(2)}, u32[]{:S(2)}) collective-permute-start(f32[2,16,16,3]{3,2,1,0:T(8,128)S(1)} %get-tuple-element.26), channel_id=1, source_target_pairs={{1,0},{3,2},{5,4},{7,6},{9,8},{11,10},{13,12},{15,14},{17,16},{19,... | collective-permute-start | bytes 18440 | tf_op jit(solution)/shard_map/ppermute | solution.py:22
  57.9 2.4 %collective-permute-done.10 = f32[2,16,16,3]{3,2,1,0:T(8,128)S(1)} collective-permute-done((f32[2,16,16,3]{3,2,1,0:T(8,128)S(1)}, f32[2,16,16,3]{3,2,1,0:T(8,128)S(1)}, u32[]{:S(2)}, u32[]{:S(2)}) %collective-permute-start.10) | collective-permute-done | bytes 6176 | tf_op jit(solution)/shard_map/ppermute | solution.py:20
  66.3 3.9 %collective-permute-start.13 = (f32[2,3,10,130]{3,2,1,0:T(8,128)S(1)}, f32[2,3,10,130]{3,2,1,0:T(8,128)S(1)}, u32[]{:S(2)}, u32[]{:S(2)}) collective-permute-start(f32[2,3,10,130]{3,2,1,0:T(8,128)S(1)} %get-tuple-element.52), channel_id=1, source_target_pairs={{8,0},{16,8},{24,16},{9,1},{17,9},{25,17},{10,2},{18,10},{26,18},{... | collective-permute-start | bytes 93608 | tf_op jit(solution)/shard_map/ppermute | solution.py:22
  70.9 1.9 %collective-permute-done.13 = f32[2,3,10,130]{3,2,1,0:T(8,128)S(1)} collective-permute-done((f32[2,3,10,130]{3,2,1,0:T(8,128)S(1)}, f32[2,3,10,130]{3,2,1,0:T(8,128)S(1)}, u32[]{:S(2)}, u32[]{:S(2)}) %collective-permute-start.13) | collective-permute-done | bytes 31232 | tf_op jit(solution)/shard_map/ppermute | solution.py:22
  74.8 3.6 %collective-permute-start.15 = (f32[2,16,3,130]{3,2,1,0:T(4,128)S(1)}, f32[2,16,3,130]{3,2,1,0:T(4,128)S(1)}, u32[]{:S(2)}, u32[]{:S(2)}) collective-permute-start(f32[2,16,3,130]{3,2,1,0:T(4,128)S(1)} %get-tuple-element.24), channel_id=1, source_target_pairs={{2,0},{4,2},{6,4},{3,1},{5,3},{7,5},{10,8},{12,10},{14,12},{11,9},... | collective-permute-start | bytes 149768 | tf_op jit(solution)/shard_map/ppermute | solution.py:22
  82.5 4.6 %collective-permute-start.17 = (f32[2,16,16,3]{3,2,1,0:T(8,128)S(1)}, f32[2,16,16,3]{3,2,1,0:T(8,128)S(1)}, u32[]{:S(2)}, u32[]{:S(2)}) collective-permute-start(f32[2,16,16,3]{3,2,1,0:T(8,128)S(1)} %get-tuple-element.22), channel_id=1, source_target_pairs={{1,0},{3,2},{5,4},{7,6},{9,8},{11,10},{13,12},{15,14},{17,16},{19,... | collective-permute-start | bytes 18440 | tf_op jit(solution)/shard_map/ppermute | solution.py:22
  87.2 2.2 %collective-permute-done.16 = f32[2,16,16,3]{3,2,1,0:T(8,128)S(1)} collective-permute-done((f32[2,16,16,3]{3,2,1,0:T(8,128)S(1)}, f32[2,16,16,3]{3,2,1,0:T(8,128)S(1)}, u32[]{:S(2)}, u32[]{:S(2)}) %collective-permute-start.16) | collective-permute-done | bytes 6176 | tf_op jit(solution)/shard_map/ppermute | solution.py:20
  95.4 3.9 %collective-permute-start.19 = (f32[2,3,10,130]{3,2,1,0:T(8,128)S(1)}, f32[2,3,10,130]{3,2,1,0:T(8,128)S(1)}, u32[]{:S(2)}, u32[]{:S(2)}) collective-permute-start(f32[2,3,10,130]{3,2,1,0:T(8,128)S(1)} %get-tuple-element.50), channel_id=1, source_target_pairs={{8,0},{16,8},{24,16},{9,1},{17,9},{25,17},{10,2},{18,10},{26,18},{... | collective-permute-start | bytes 93608 | tf_op jit(solution)/shard_map/ppermute | solution.py:22
  100.0 1.9 %collective-permute-done.19 = f32[2,3,10,130]{3,2,1,0:T(8,128)S(1)} collective-permute-done((f32[2,3,10,130]{3,2,1,0:T(8,128)S(1)}, f32[2,3,10,130]{3,2,1,0:T(8,128)S(1)}, u32[]{:S(2)}, u32[]{:S(2)}) %collective-permute-start.19) | collective-permute-done | bytes 31232 | tf_op jit(solution)/shard_map/ppermute | solution.py:22
  102.0 1.9 %collective-permute-start.20 = (f32[2,16,3,130]{3,2,1,0:T(4,128)S(1)}, f32[2,16,3,130]{3,2,1,0:T(4,128)S(1)}, u32[]{:S(2)}, u32[]{:S(2)}) collective-permute-start(f32[2,16,3,130]{3,2,1,0:T(4,128)S(1)} %get-tuple-element.19), channel_id=1, source_target_pairs={{0,2},{2,4},{4,6},{1,3},{3,5},{5,7},{8,10},{10,12},{12,14},{9,11},... | collective-permute-start | bytes 149768 | tf_op jit(solution)/shard_map/ppermute | solution.py:20
  103.9 3.6 %collective-permute-start.21 = (f32[2,16,3,130]{3,2,1,0:T(4,128)S(1)}, f32[2,16,3,130]{3,2,1,0:T(4,128)S(1)}, u32[]{:S(2)}, u32[]{:S(2)}) collective-permute-start(f32[2,16,3,130]{3,2,1,0:T(4,128)S(1)} %get-tuple-element.20), channel_id=1, source_target_pairs={{2,0},{4,2},{6,4},{3,1},{5,3},{7,5},{10,8},{12,10},{14,12},{11,9},... | collective-permute-start | bytes 149768 | tf_op jit(solution)/shard_map/ppermute | solution.py:22
  111.6 4.8 %collective-permute-start.23 = (f32[2,16,16,3]{3,2,1,0:T(8,128)S(1)}, f32[2,16,16,3]{3,2,1,0:T(8,128)S(1)}, u32[]{:S(2)}, u32[]{:S(2)}) collective-permute-start(f32[2,16,16,3]{3,2,1,0:T(8,128)S(1)} %get-tuple-element.18), channel_id=1, source_target_pairs={{1,0},{3,2},{5,4},{7,6},{9,8},{11,10},{13,12},{15,14},{17,16},{19,... | collective-permute-start | bytes 18440 | tf_op jit(solution)/shard_map/ppermute | solution.py:22
  116.5 2.1 %collective-permute-done.22 = f32[2,16,16,3]{3,2,1,0:T(8,128)S(1)} collective-permute-done((f32[2,16,16,3]{3,2,1,0:T(8,128)S(1)}, f32[2,16,16,3]{3,2,1,0:T(8,128)S(1)}, u32[]{:S(2)}, u32[]{:S(2)}) %collective-permute-start.22) | collective-permute-done | bytes 6176 | tf_op jit(solution)/shard_map/ppermute | solution.py:20
  124.6 3.9 %collective-permute-start.25 = (f32[2,3,10,130]{3,2,1,0:T(8,128)S(1)}, f32[2,3,10,130]{3,2,1,0:T(8,128)S(1)}, u32[]{:S(2)}, u32[]{:S(2)}) collective-permute-start(f32[2,3,10,130]{3,2,1,0:T(8,128)S(1)} %get-tuple-element.48), channel_id=1, source_target_pairs={{8,0},{16,8},{24,16},{9,1},{17,9},{25,17},{10,2},{18,10},{26,18},{... | collective-permute-start | bytes 93608 | tf_op jit(solution)/shard_map/ppermute | solution.py:22
  129.2 1.9 %collective-permute-done.25 = f32[2,3,10,130]{3,2,1,0:T(8,128)S(1)} collective-permute-done((f32[2,3,10,130]{3,2,1,0:T(8,128)S(1)}, f32[2,3,10,130]{3,2,1,0:T(8,128)S(1)}, u32[]{:S(2)}, u32[]{:S(2)}) %collective-permute-start.25) | collective-permute-done | bytes 31232 | tf_op jit(solution)/shard_map/ppermute | solution.py:22
  133.1 3.6 %collective-permute-start.27 = (f32[2,16,3,130]{3,2,1,0:T(4,128)S(1)}, f32[2,16,3,130]{3,2,1,0:T(4,128)S(1)}, u32[]{:S(2)}, u32[]{:S(2)}) collective-permute-start(f32[2,16,3,130]{3,2,1,0:T(4,128)S(1)} %get-tuple-element.16), channel_id=1, source_target_pairs={{2,0},{4,2},{6,4},{3,1},{5,3},{7,5},{10,8},{12,10},{14,12},{11,9},... | collective-permute-start | bytes 149768 | tf_op jit(solution)/shard_map/ppermute | solution.py:22
  140.8 4.6 %collective-permute-start.29 = (f32[2,16,16,3]{3,2,1,0:T(8,128)S(1)}, f32[2,16,16,3]{3,2,1,0:T(8,128)S(1)}, u32[]{:S(2)}, u32[]{:S(2)}) collective-permute-start(f32[2,16,16,3]{3,2,1,0:T(8,128)S(1)} %get-tuple-element.14), channel_id=1, source_target_pairs={{1,0},{3,2},{5,4},{7,6},{9,8},{11,10},{13,12},{15,14},{17,16},{19,... | collective-permute-start | bytes 18440 | tf_op jit(solution)/shard_map/ppermute | solution.py:22
  145.5 2.3 %collective-permute-done.28 = f32[2,16,16,3]{3,2,1,0:T(8,128)S(1)} collective-permute-done((f32[2,16,16,3]{3,2,1,0:T(8,128)S(1)}, f32[2,16,16,3]{3,2,1,0:T(8,128)S(1)}, u32[]{:S(2)}, u32[]{:S(2)}) %collective-permute-start.28) | collective-permute-done | bytes 6176 | tf_op jit(solution)/shard_map/ppermute | solution.py:20
  153.3 15.3 %all-reduce.39 = (f32[9,9]{1,0:T(8,128)S(1)}, f32[9]{0:T(128)S(1)}) all-reduce(f32[9,9]{1,0:T(8,128)S(1)} %fusion.151, f32[9]{0:T(128)S(1)} %convolution_bitcast_fusion), channel_id=1, replica_groups=mesh['gx'=4,'gy'=4,'gz'=2] {'gy','gz'}, use_global_device_ids=true, to_apply=%region_0.1 | all-reduce | flops 90 | bytes 720 | tf_op jit(solution)/shard_map/psum | solution.py:150
  168.6 10.6 %all-reduce.40 = (f32[9,9]{1,0:T(8,128)S(1)}, f32[9]{0:T(128)S(1)}) all-reduce(f32[9,9]{1,0:T(8,128)S(1)} %get-tuple-element.3, f32[9]{0:T(128)S(1)} %get-tuple-element.4), channel_id=1, replica_groups=mesh['gx'=4,'gy'=4,'gz'=2] {'gx'}, use_global_device_ids=true, to_apply=%region_1.2 | all-reduce | flops 90 | bytes 720 | tf_op jit(solution)/shard_map/psum | solution.py:149
  (141 shorter events, 59.1 us)
Async XLA Ops:
  1.6 6.5 %collective-permute-start = (f32[2,3,10,130]{3,2,1,0:T(8,128)S(1)}, f32[2,3,10,130]{3,2,1,0:T(8,128)S(1)}, u32[]{:S(2)}, u32[]{:S(2)}) collective-permute-start(f32[2,3,10,130]{3,2,1,0:T(8,128)S(1)} %get-tuple-element.55), channel_id=1, source_target_pairs={{0,8},{8,16},{16,24},{1,9},{9,17},{17,25},{2,10},{10,18},{18,26},{... | collective-permute-start | bytes 93608 | tf_op jit(solution)/shard_map/ppermute | solution.py:20
  5.1 6.5 %collective-permute-start.1 = (f32[2,3,10,130]{3,2,1,0:T(8,128)S(1)}, f32[2,3,10,130]{3,2,1,0:T(8,128)S(1)}, u32[]{:S(2)}, u32[]{:S(2)}) collective-permute-start(f32[2,3,10,130]{3,2,1,0:T(8,128)S(1)} %get-tuple-element.56), channel_id=1, source_target_pairs={{8,0},{16,8},{24,16},{9,1},{17,9},{25,17},{10,2},{18,10},{26,18},{... | collective-permute-start | bytes 93608 | tf_op jit(solution)/shard_map/ppermute | solution.py:22
  11.6 6.3 %collective-permute-start.2 = (f32[2,16,3,130]{3,2,1,0:T(4,128)S(1)}, f32[2,16,3,130]{3,2,1,0:T(4,128)S(1)}, u32[]{:S(2)}, u32[]{:S(2)}) collective-permute-start(f32[2,16,3,130]{3,2,1,0:T(4,128)S(1)} %get-tuple-element.31), channel_id=1, source_target_pairs={{0,2},{2,4},{4,6},{1,3},{3,5},{5,7},{8,10},{10,12},{12,14},{9,11},... | collective-permute-start | bytes 149768 | tf_op jit(solution)/shard_map/ppermute | solution.py:20
  13.6 6.1 %collective-permute-start.3 = (f32[2,16,3,130]{3,2,1,0:T(4,128)S(1)}, f32[2,16,3,130]{3,2,1,0:T(4,128)S(1)}, u32[]{:S(2)}, u32[]{:S(2)}) collective-permute-start(f32[2,16,3,130]{3,2,1,0:T(4,128)S(1)} %get-tuple-element.32), channel_id=1, source_target_pairs={{2,0},{4,2},{6,4},{3,1},{5,3},{7,5},{10,8},{12,10},{14,12},{11,9},... | collective-permute-start | bytes 149768 | tf_op jit(solution)/shard_map/ppermute | solution.py:22
  20.0 8.3 %collective-permute-start.4 = (f32[2,16,16,3]{3,2,1,0:T(8,128)S(1)}, f32[2,16,16,3]{3,2,1,0:T(8,128)S(1)}, u32[]{:S(2)}, u32[]{:S(2)}) collective-permute-start(f32[2,16,16,3]{3,2,1,0:T(8,128)S(1)} %get-tuple-element.29), channel_id=1, source_target_pairs={{0,1},{2,3},{4,5},{6,7},{8,9},{10,11},{12,13},{14,15},{16,17},{18,... | collective-permute-start | bytes 18440 | tf_op jit(solution)/shard_map/ppermute | solution.py:20
  21.3 8.4 %collective-permute-start.5 = (f32[2,16,16,3]{3,2,1,0:T(8,128)S(1)}, f32[2,16,16,3]{3,2,1,0:T(8,128)S(1)}, u32[]{:S(2)}, u32[]{:S(2)}) collective-permute-start(f32[2,16,16,3]{3,2,1,0:T(8,128)S(1)} %get-tuple-element.30), channel_id=1, source_target_pairs={{1,0},{3,2},{5,4},{7,6},{9,8},{11,10},{13,12},{15,14},{17,16},{19,... | collective-permute-start | bytes 18440 | tf_op jit(solution)/shard_map/ppermute | solution.py:22
  31.3 0.7 copy-start.2
  33.6 6.5 %collective-permute-start.6 = (f32[2,3,10,130]{3,2,1,0:T(8,128)S(1)}, f32[2,3,10,130]{3,2,1,0:T(8,128)S(1)}, u32[]{:S(2)}, u32[]{:S(2)}) collective-permute-start(f32[2,3,10,130]{3,2,1,0:T(8,128)S(1)} %get-tuple-element.53), channel_id=1, source_target_pairs={{0,8},{8,16},{16,24},{1,9},{9,17},{17,25},{2,10},{10,18},{18,26},{... | collective-permute-start | bytes 93608 | tf_op jit(solution)/shard_map/ppermute | solution.py:20
  37.1 6.5 %collective-permute-start.7 = (f32[2,3,10,130]{3,2,1,0:T(8,128)S(1)}, f32[2,3,10,130]{3,2,1,0:T(8,128)S(1)}, u32[]{:S(2)}, u32[]{:S(2)}) collective-permute-start(f32[2,3,10,130]{3,2,1,0:T(8,128)S(1)} %get-tuple-element.54), channel_id=1, source_target_pairs={{8,0},{16,8},{24,16},{9,1},{17,9},{25,17},{10,2},{18,10},{26,18},{... | collective-permute-start | bytes 93608 | tf_op jit(solution)/shard_map/ppermute | solution.py:22
  43.7 6.3 %collective-permute-start.8 = (f32[2,16,3,130]{3,2,1,0:T(4,128)S(1)}, f32[2,16,3,130]{3,2,1,0:T(4,128)S(1)}, u32[]{:S(2)}, u32[]{:S(2)}) collective-permute-start(f32[2,16,3,130]{3,2,1,0:T(4,128)S(1)} %get-tuple-element.27), channel_id=1, source_target_pairs={{0,2},{2,4},{4,6},{1,3},{3,5},{5,7},{8,10},{10,12},{12,14},{9,11},... | collective-permute-start | bytes 149768 | tf_op jit(solution)/shard_map/ppermute | solution.py:20
  45.6 6.1 %collective-permute-start.9 = (f32[2,16,3,130]{3,2,1,0:T(4,128)S(1)}, f32[2,16,3,130]{3,2,1,0:T(4,128)S(1)}, u32[]{:S(2)}, u32[]{:S(2)}) collective-permute-start(f32[2,16,3,130]{3,2,1,0:T(4,128)S(1)} %get-tuple-element.28), channel_id=1, source_target_pairs={{2,0},{4,2},{6,4},{3,1},{5,3},{7,5},{10,8},{12,10},{14,12},{11,9},... | collective-permute-start | bytes 149768 | tf_op jit(solution)/shard_map/ppermute | solution.py:22
  52.0 8.3 %collective-permute-start.10 = (f32[2,16,16,3]{3,2,1,0:T(8,128)S(1)}, f32[2,16,16,3]{3,2,1,0:T(8,128)S(1)}, u32[]{:S(2)}, u32[]{:S(2)}) collective-permute-start(f32[2,16,16,3]{3,2,1,0:T(8,128)S(1)} %get-tuple-element.25), channel_id=1, source_target_pairs={{0,1},{2,3},{4,5},{6,7},{8,9},{10,11},{12,13},{14,15},{16,17},{18,... | collective-permute-start | bytes 18440 | tf_op jit(solution)/shard_map/ppermute | solution.py:20
  53.3 8.4 %collective-permute-start.11 = (f32[2,16,16,3]{3,2,1,0:T(8,128)S(1)}, f32[2,16,16,3]{3,2,1,0:T(8,128)S(1)}, u32[]{:S(2)}, u32[]{:S(2)}) collective-permute-start(f32[2,16,16,3]{3,2,1,0:T(8,128)S(1)} %get-tuple-element.26), channel_id=1, source_target_pairs={{1,0},{3,2},{5,4},{7,6},{9,8},{11,10},{13,12},{15,14},{17,16},{19,... | collective-permute-start | bytes 18440 | tf_op jit(solution)/shard_map/ppermute | solution.py:22
  64.3 6.5 %collective-permute-start.12 = (f32[2,3,10,130]{3,2,1,0:T(8,128)S(1)}, f32[2,3,10,130]{3,2,1,0:T(8,128)S(1)}, u32[]{:S(2)}, u32[]{:S(2)}) collective-permute-start(f32[2,3,10,130]{3,2,1,0:T(8,128)S(1)} %get-tuple-element.51), channel_id=1, source_target_pairs={{0,8},{8,16},{16,24},{1,9},{9,17},{17,25},{2,10},{10,18},{18,26},{... | collective-permute-start | bytes 93608 | tf_op jit(solution)/shard_map/ppermute | solution.py:20
  66.3 6.5 %collective-permute-start.13 = (f32[2,3,10,130]{3,2,1,0:T(8,128)S(1)}, f32[2,3,10,130]{3,2,1,0:T(8,128)S(1)}, u32[]{:S(2)}, u32[]{:S(2)}) collective-permute-start(f32[2,3,10,130]{3,2,1,0:T(8,128)S(1)} %get-tuple-element.52), channel_id=1, source_target_pairs={{8,0},{16,8},{24,16},{9,1},{17,9},{25,17},{10,2},{18,10},{26,18},{... | collective-permute-start | bytes 93608 | tf_op jit(solution)/shard_map/ppermute | solution.py:22
  72.8 6.3 %collective-permute-start.14 = (f32[2,16,3,130]{3,2,1,0:T(4,128)S(1)}, f32[2,16,3,130]{3,2,1,0:T(4,128)S(1)}, u32[]{:S(2)}, u32[]{:S(2)}) collective-permute-start(f32[2,16,3,130]{3,2,1,0:T(4,128)S(1)} %get-tuple-element.23), channel_id=1, source_target_pairs={{0,2},{2,4},{4,6},{1,3},{3,5},{5,7},{8,10},{10,12},{12,14},{9,11},... | collective-permute-start | bytes 149768 | tf_op jit(solution)/shard_map/ppermute | solution.py:20
  74.8 6.1 %collective-permute-start.15 = (f32[2,16,3,130]{3,2,1,0:T(4,128)S(1)}, f32[2,16,3,130]{3,2,1,0:T(4,128)S(1)}, u32[]{:S(2)}, u32[]{:S(2)}) collective-permute-start(f32[2,16,3,130]{3,2,1,0:T(4,128)S(1)} %get-tuple-element.24), channel_id=1, source_target_pairs={{2,0},{4,2},{6,4},{3,1},{5,3},{7,5},{10,8},{12,10},{14,12},{11,9},... | collective-permute-start | bytes 149768 | tf_op jit(solution)/shard_map/ppermute | solution.py:22
  81.2 8.3 %collective-permute-start.16 = (f32[2,16,16,3]{3,2,1,0:T(8,128)S(1)}, f32[2,16,16,3]{3,2,1,0:T(8,128)S(1)}, u32[]{:S(2)}, u32[]{:S(2)}) collective-permute-start(f32[2,16,16,3]{3,2,1,0:T(8,128)S(1)} %get-tuple-element.21), channel_id=1, source_target_pairs={{0,1},{2,3},{4,5},{6,7},{8,9},{10,11},{12,13},{14,15},{16,17},{18,... | collective-permute-start | bytes 18440 | tf_op jit(solution)/shard_map/ppermute | solution.py:20
  82.5 8.4 %collective-permute-start.17 = (f32[2,16,16,3]{3,2,1,0:T(8,128)S(1)}, f32[2,16,16,3]{3,2,1,0:T(8,128)S(1)}, u32[]{:S(2)}, u32[]{:S(2)}) collective-permute-start(f32[2,16,16,3]{3,2,1,0:T(8,128)S(1)} %get-tuple-element.22), channel_id=1, source_target_pairs={{1,0},{3,2},{5,4},{7,6},{9,8},{11,10},{13,12},{15,14},{17,16},{19,... | collective-permute-start | bytes 18440 | tf_op jit(solution)/shard_map/ppermute | solution.py:22
  93.5 6.5 %collective-permute-start.18 = (f32[2,3,10,130]{3,2,1,0:T(8,128)S(1)}, f32[2,3,10,130]{3,2,1,0:T(8,128)S(1)}, u32[]{:S(2)}, u32[]{:S(2)}) collective-permute-start(f32[2,3,10,130]{3,2,1,0:T(8,128)S(1)} %get-tuple-element.49), channel_id=1, source_target_pairs={{0,8},{8,16},{16,24},{1,9},{9,17},{17,25},{2,10},{10,18},{18,26},{... | collective-permute-start | bytes 93608 | tf_op jit(solution)/shard_map/ppermute | solution.py:20
  95.4 6.5 %collective-permute-start.19 = (f32[2,3,10,130]{3,2,1,0:T(8,128)S(1)}, f32[2,3,10,130]{3,2,1,0:T(8,128)S(1)}, u32[]{:S(2)}, u32[]{:S(2)}) collective-permute-start(f32[2,3,10,130]{3,2,1,0:T(8,128)S(1)} %get-tuple-element.50), channel_id=1, source_target_pairs={{8,0},{16,8},{24,16},{9,1},{17,9},{25,17},{10,2},{18,10},{26,18},{... | collective-permute-start | bytes 93608 | tf_op jit(solution)/shard_map/ppermute | solution.py:22
  102.0 6.3 %collective-permute-start.20 = (f32[2,16,3,130]{3,2,1,0:T(4,128)S(1)}, f32[2,16,3,130]{3,2,1,0:T(4,128)S(1)}, u32[]{:S(2)}, u32[]{:S(2)}) collective-permute-start(f32[2,16,3,130]{3,2,1,0:T(4,128)S(1)} %get-tuple-element.19), channel_id=1, source_target_pairs={{0,2},{2,4},{4,6},{1,3},{3,5},{5,7},{8,10},{10,12},{12,14},{9,11},... | collective-permute-start | bytes 149768 | tf_op jit(solution)/shard_map/ppermute | solution.py:20
  103.9 6.1 %collective-permute-start.21 = (f32[2,16,3,130]{3,2,1,0:T(4,128)S(1)}, f32[2,16,3,130]{3,2,1,0:T(4,128)S(1)}, u32[]{:S(2)}, u32[]{:S(2)}) collective-permute-start(f32[2,16,3,130]{3,2,1,0:T(4,128)S(1)} %get-tuple-element.20), channel_id=1, source_target_pairs={{2,0},{4,2},{6,4},{3,1},{5,3},{7,5},{10,8},{12,10},{14,12},{11,9},... | collective-permute-start | bytes 149768 | tf_op jit(solution)/shard_map/ppermute | solution.py:22
  110.3 8.3 %collective-permute-start.22 = (f32[2,16,16,3]{3,2,1,0:T(8,128)S(1)}, f32[2,16,16,3]{3,2,1,0:T(8,128)S(1)}, u32[]{:S(2)}, u32[]{:S(2)}) collective-permute-start(f32[2,16,16,3]{3,2,1,0:T(8,128)S(1)} %get-tuple-element.17), channel_id=1, source_target_pairs={{0,1},{2,3},{4,5},{6,7},{8,9},{10,11},{12,13},{14,15},{16,17},{18,... | collective-permute-start | bytes 18440 | tf_op jit(solution)/shard_map/ppermute | solution.py:20
  111.6 8.4 %collective-permute-start.23 = (f32[2,16,16,3]{3,2,1,0:T(8,128)S(1)}, f32[2,16,16,3]{3,2,1,0:T(8,128)S(1)}, u32[]{:S(2)}, u32[]{:S(2)}) collective-permute-start(f32[2,16,16,3]{3,2,1,0:T(8,128)S(1)} %get-tuple-element.18), channel_id=1, source_target_pairs={{1,0},{3,2},{5,4},{7,6},{9,8},{11,10},{13,12},{15,14},{17,16},{19,... | collective-permute-start | bytes 18440 | tf_op jit(solution)/shard_map/ppermute | solution.py:22
  122.7 6.5 %collective-permute-start.24 = (f32[2,3,10,130]{3,2,1,0:T(8,128)S(1)}, f32[2,3,10,130]{3,2,1,0:T(8,128)S(1)}, u32[]{:S(2)}, u32[]{:S(2)}) collective-permute-start(f32[2,3,10,130]{3,2,1,0:T(8,128)S(1)} %get-tuple-element.47), channel_id=1, source_target_pairs={{0,8},{8,16},{16,24},{1,9},{9,17},{17,25},{2,10},{10,18},{18,26},{... | collective-permute-start | bytes 93608 | tf_op jit(solution)/shard_map/ppermute | solution.py:20
  124.6 6.5 %collective-permute-start.25 = (f32[2,3,10,130]{3,2,1,0:T(8,128)S(1)}, f32[2,3,10,130]{3,2,1,0:T(8,128)S(1)}, u32[]{:S(2)}, u32[]{:S(2)}) collective-permute-start(f32[2,3,10,130]{3,2,1,0:T(8,128)S(1)} %get-tuple-element.48), channel_id=1, source_target_pairs={{8,0},{16,8},{24,16},{9,1},{17,9},{25,17},{10,2},{18,10},{26,18},{... | collective-permute-start | bytes 93608 | tf_op jit(solution)/shard_map/ppermute | solution.py:22
  131.2 6.3 %collective-permute-start.26 = (f32[2,16,3,130]{3,2,1,0:T(4,128)S(1)}, f32[2,16,3,130]{3,2,1,0:T(4,128)S(1)}, u32[]{:S(2)}, u32[]{:S(2)}) collective-permute-start(f32[2,16,3,130]{3,2,1,0:T(4,128)S(1)} %get-tuple-element.15), channel_id=1, source_target_pairs={{0,2},{2,4},{4,6},{1,3},{3,5},{5,7},{8,10},{10,12},{12,14},{9,11},... | collective-permute-start | bytes 149768 | tf_op jit(solution)/shard_map/ppermute | solution.py:20
  133.1 6.1 %collective-permute-start.27 = (f32[2,16,3,130]{3,2,1,0:T(4,128)S(1)}, f32[2,16,3,130]{3,2,1,0:T(4,128)S(1)}, u32[]{:S(2)}, u32[]{:S(2)}) collective-permute-start(f32[2,16,3,130]{3,2,1,0:T(4,128)S(1)} %get-tuple-element.16), channel_id=1, source_target_pairs={{2,0},{4,2},{6,4},{3,1},{5,3},{7,5},{10,8},{12,10},{14,12},{11,9},... | collective-permute-start | bytes 149768 | tf_op jit(solution)/shard_map/ppermute | solution.py:22
  139.5 8.3 %collective-permute-start.28 = (f32[2,16,16,3]{3,2,1,0:T(8,128)S(1)}, f32[2,16,16,3]{3,2,1,0:T(8,128)S(1)}, u32[]{:S(2)}, u32[]{:S(2)}) collective-permute-start(f32[2,16,16,3]{3,2,1,0:T(8,128)S(1)} %get-tuple-element.13), channel_id=1, source_target_pairs={{0,1},{2,3},{4,5},{6,7},{8,9},{10,11},{12,13},{14,15},{16,17},{18,... | collective-permute-start | bytes 18440 | tf_op jit(solution)/shard_map/ppermute | solution.py:20
  140.8 8.4 %collective-permute-start.29 = (f32[2,16,16,3]{3,2,1,0:T(8,128)S(1)}, f32[2,16,16,3]{3,2,1,0:T(8,128)S(1)}, u32[]{:S(2)}, u32[]{:S(2)}) collective-permute-start(f32[2,16,16,3]{3,2,1,0:T(8,128)S(1)} %get-tuple-element.14), channel_id=1, source_target_pairs={{1,0},{3,2},{5,4},{7,6},{9,8},{11,10},{13,12},{15,14},{17,16},{19,... | collective-permute-start | bytes 18440 | tf_op jit(solution)/shard_map/ppermute | solution.py:22
  151.8 0.8 copy-start
  (1 other events, 0.7 us)
